TPU v7x, 256 devices: a whole 4x4x8 slice. The times are simulated.
256 devices in a mesh: span: 64 (over y, x, z_lo, core), head: 4 (over z_hi).
Axes of the slice: x: 4, y: 4, z: 8 (z_hi: 4, z_lo: 2; z = z_hi * 2 + z_lo), core: 2. Of those that a mesh axis runs over, the one named last changes fastest.
Arguments:
- decoder_states: bfloat16 [131072, 1024], P('span'), may hold values from -21 to 21
- encodings: bfloat16 [4096, 128, 1024], P('span', 'head'), may hold values from -21 to 21
- neighbor_table: int32 [2048, 2, 2], P('span'), may hold values from 0 to 63, as said below
- query_weight: bfloat16 [1024, 1024], P(None, 'head'), may hold values from -0.1875 to 0.1875
- key_weight: bfloat16 [1024, 1024], P(None, 'head'), may hold values from -0.1875 to 0.1875
- value_weight: bfloat16 [1024, 1024], P(None, 'head'), may hold values from -0.1875 to 0.1875
- out_weight: bfloat16 [1024, 1024], P('head'), may hold values from -0.1875 to 0.1875
Outputs:
- attended: bfloat16 [131072, 1024], P('span', 'head')
Inputs may be any that keep to these rules, and one draw needn't show every extreme that they name: neighbor_table[c, k, 0] is the database shard and neighbor_table[c, k, 1] the slot in that shard of neighbor k of span c; in each aligned block of 32 spans (the spans of one device along `span`) every shard is named by exactly one neighbor, and every slot of every shard is named exactly once in the whole table.
All inputs are finite; a program needn't handle non-finite values.
Results may differ from a plain program's by a relative error of at most 0.012.
The roundings to bfloat16 on the way count: a program that leaves them out, or rounds other values in their place, can miss the bound.
Values may be sent and summed in bfloat16 or wider, within the bound.
A program may use at most 128 MiB of HBM per device.

v0:
```python
import jax
import jax.numpy as jnp
from jax import lax
from jax.sharding import PartitionSpec as P

HEAD_DIM = 64
SPAN_LEN = 64
SEQ_LEN = 2048


def body(
    decoder_states, encodings, neighbor_table, query_weight, key_weight, value_weight, out_weight
):
    peer_count = lax.axis_size("span")
    column_rows = lax.all_to_all(out_weight, "head", split_axis=1, concat_axis=0, tiled=True)
    shard_ids = neighbor_table[:, :, 0].reshape(-1)
    slot_ids = neighbor_table[:, :, 1].reshape(-1)
    entries = shard_ids.shape[0]
    per_peer = entries // peer_count
    numbering = jnp.arange(entries, dtype=jnp.int32)
    same_before = (shard_ids[:, None] == shard_ids[None, :]) & (
        numbering[None, :] < numbering[:, None]
    )
    ranking = jnp.sum(same_before.astype(jnp.int32), axis=1)
    position = shard_ids * per_peer + ranking
    placed = position[None, :] == numbering[:, None]
    request = jnp.sum(jnp.where(placed, slot_ids[None, :], 0), axis=1)
    wanted = lax.all_to_all(request, "span", split_axis=0, concat_axis=0, tiled=True)
    selected = encodings[wanted]
    model_width = decoder_states.shape[1]
    group_cols = query_weight.shape[1]
    both_weights = jnp.concatenate([key_weight, value_weight], axis=1)
    arrived = lax.all_to_all(selected, "span", split_axis=0, concat_axis=0, tiled=True)
    block_in = lax.all_gather(arrived, "head", axis=1, tiled=True)
    flattened = block_in.reshape(-1, model_width)
    result = jnp.dot(flattened, both_weights, preferred_element_type=jnp.float32).astype(
        jnp.bfloat16
    )
    projected = result.reshape(block_in.shape[0], block_in.shape[1], 2 * group_cols)
    ordered = projected[position]
    span_count = neighbor_table.shape[0]
    neighbors = neighbor_table.shape[1]
    heads_here = group_cols // HEAD_DIM
    ordered = ordered.reshape(span_count, neighbors * projected.shape[1], 2 * group_cols)
    key_rows = ordered[:, :, :group_cols].reshape(span_count, -1, heads_here, HEAD_DIM)
    value_rows = ordered[:, :, group_cols:].reshape(span_count, -1, heads_here, HEAD_DIM)
    queries = jnp.dot(decoder_states, query_weight, preferred_element_type=jnp.float32).astype(
        jnp.bfloat16
    )
    sequences = decoder_states.shape[0] // SEQ_LEN
    offset = SPAN_LEN - 1
    queries = queries.reshape(sequences, SEQ_LEN, group_cols)
    shifted = jnp.concatenate(
        [queries[:, offset:], jnp.zeros((sequences, offset, group_cols), jnp.bfloat16)], axis=1
    )
    shifted = shifted.reshape(span_count, SPAN_LEN, heads_here, HEAD_DIM)
    inv_root = HEAD_DIM ** (-0.5)
    scores = (
        jnp.einsum("cqhd,ckhd->chqk", shifted, key_rows, preferred_element_type=jnp.float32)
        * inv_root
    )
    weights = jax.nn.softmax(scores, axis=-1).astype(jnp.bfloat16)
    context = jnp.einsum(
        "chqk,ckhd->cqhd", weights, value_rows, preferred_element_type=jnp.float32
    ).astype(jnp.bfloat16)
    context = context.reshape(sequences, SEQ_LEN, group_cols)
    context = jnp.concatenate(
        [jnp.zeros((sequences, offset, group_cols), jnp.bfloat16), context[:, : SEQ_LEN - offset]],
        axis=1,
    )
    context = context.reshape(-1, group_cols)
    summed = jnp.dot(
        lax.all_gather(context, "head", axis=1, tiled=True),
        column_rows,
        preferred_element_type=jnp.float32,
    )
    return summed.astype(jnp.bfloat16)


def solution(mesh):
    return jax.shard_map(
        body,
        mesh=mesh,
        in_specs=(
            P("span", None),
            P("span", "head", None),
            P("span", None, None),
            P(None, "head"),
            P(None, "head"),
            P(None, "head"),
            P("head", None),
        ),
        out_specs=P("span", "head"),
        check_vma=False,
    )
```

profile of v0, /device:TPU:33, one launch (start us, length us, event | category | flops | bytes accessed | tf_op | source)
XLA Modules:
  0.0 560.3 jit_solution(16839109739039627777)
XLA Ops:
  6.5 0.0 copy-start
  6.5 0.0 all-gather.4.cloned.1.call-start
  6.5 0.8 fusion.30
  7.3 0.1 copy.50
  7.4 0.1 reshape_squeeze.5
  7.5 0.2 convert_reduce_fusion
  7.7 0.1 copy.51
  7.8 0.1 broadcast_in_dim.14
  7.9 0.1 select_reduce_fusion
  8.0 0.1 copy.52
  8.1 15.8 %all_to_all.36 = s32[64,1,1]{2,1,0:T(1,128)S(1)} all-to-all(s32[64,1,1]{2,1,0:T(1,128)S(1)} %copy.52), channel_id=1, replica_groups=mesh['span'=64,'head'=4] {'span'}, dimensions={0} | all-to-all | bytes 512 | tf_op jit(solution)/shard_map/all_to_all | solution.py:28
  23.9 1.2 reduce
  25.1 4.9 gather_fusion
  30.1 56.3 %all_to_all.37 = bf16[64,32,1024]{2,1,0:T(8,128)(2,1)} all-to-all(bf16[64,32,1024]{2,1,0:T(8,128)(2,1)} %gather_fusion), channel_id=1, replica_groups=mesh['span'=64,'head'=4] {'span'}, dimensions={0} | all-to-all | bytes 8388608 | tf_op jit(solution)/shard_map/all_to_all | solution.py:33
  86.4 0.0 all-gather.4.cloned.1.call-update
  86.4 0.2 all-gather.6.cloned.1.call-start
  86.6 0.1 reshape_squeeze.6
  86.7 0.0 copy-done
  86.7 3.4 fusion.11
  90.2 0.0 copy-start.4
  90.2 0.2 slice.29
  90.4 1.0 concatenate.10
  91.5 3.3 reshape.100
  94.8 285.4 %all-gather.4.cloned.1.call-done = bf16[64,128,1024]{2,1,0:T(8,128)(2,1)} async-done(((bf16[64,32,1024]{2,1,0:T(8,128)(2,1)}), bf16[64,128,1024]{2,1,0:T(8,128)(2,1)}) %all-gather.4.cloned.1.call-update) | async-done | bytes 16777232 | tf_op jit(solution)/shard_map/all_gather | solution.py:34
  380.3 0.0 copy-done.4
  380.3 14.5 %convolution_convert_fusion = bf16[8192,512]{1,0:T(8,128)(2,1)} fusion(bf16[8192,1024]{1,0:T(8,128)(2,1)} %bitcast.54, bf16[1024,256]{1,0:T(8,128)(2,1)S(1)} %copy-done.4, bf16[1024,256]{1,0:T(8,128)(2,1)} %param.11), kind=kOutput, calls=%fused_computation.3 | convolution fusion | flops 8596226048 | bytes 26214400 | tf_op jit(solution)/shard_map/dot_general | solution.py:36
  394.8 8.9 %gather_fusion.1 = bf16[64,128,512]{2,1,0:T(8,128)(2,1)} fusion(bf16[64,128,512]{2,1,0:T(8,128)(2,1)} %bitcast.47, s32[1024]{0:T(1024)S(1)} %pad_clamp_fusion), kind=kCustom, calls=%fused_computation.1 | custom fusion | bytes 16777472 | tf_op jit(solution)/shard_map/gather | solution.py:40
  403.7 5.9 %fusion.29 = (bf16[32,256,256]{2,1,0:T(8,128)(2,1)}, bf16[32,256,256]{2,1,0:T(8,128)(2,1)}) fusion(bf16[32,256,512]{2,1,0:T(8,128)(2,1)} %bitcast.45), kind=kLoop, calls=%fused_computation.37 | loop fusion | bytes 16777216 | tf_op jit(solution)/shard_map/slice | solution.py:45
  409.6 6.4 %copy.61 = bf16[32,256,256]{1,2,0:T(8,128)(2,1)} copy(bf16[32,256,256]{2,1,0:T(8,128)(2,1)} %get-tuple-element.5) | data formatting | bytes 8388608
  416.0 3.4 fusion.12
  419.4 0.0 copy-start.2
  419.4 3.1 fusion.31
  422.6 0.1 copy-done.2
  422.6 6.4 %copy.60 = bf16[32,256,256]{1,2,0:T(8,128)(2,1)} copy(bf16[32,256,256]{2,1,0:T(8,128)(2,1)} %get-tuple-element.6) | data formatting | bytes 8388608
  429.0 22.4 %convert_bitcast_fusion = bf16[32,64,4,64]{1,3,2,0:T(8,128)(2,1)} fusion(bf16[32,256,4,64]{1,3,2,0:T(8,128)(2,1)} %bitcast.49, f32[32,4,64]{2,1,0:T(4,128)S(1)} %fusion.31, f32[32,4,64,256]{3,2,1,0:T(8,128)} %copy-done.2), kind=kOutput, calls=%fused_computation.17 | convolution fusion | flops 279453952 | bytes 13664256 | tf_op jit(solution)/shard_map/chqk,ckhd->cqhd/dot_general | solution.py:63
  451.4 2.9 copy.57
  454.4 0.0 copy-start.3
  454.4 2.4 reshape.102
  456.8 2.6 concatenate.11
  459.4 0.0 all-gather.6.cloned.1.call-update
  459.5 0.0 copy-done.3
  459.5 0.2 copy.58
  459.7 16.1 %all_to_all.38 = bf16[256,4,256]{0,2,1:T(8,128)(2,1)S(1)} all-to-all(bf16[256,4,256]{0,2,1:T(8,128)(2,1)S(1)} %bitcast.51), channel_id=1, replica_groups=mesh['span'=64,'head'=4] {'head'}, dimensions={1} | all-to-all | bytes 1048576 | tf_op jit(solution)/shard_map/all_to_all | solution.py:15
  475.8 0.2 copy.59
  476.0 72.9 %all-gather.6.cloned.1.call-done = bf16[1,2048,1024]{1,2,0:T(8,128)(2,1)} async-done(((bf16[1,2048,256]{1,2,0:T(8,128)(2,1)}), bf16[1,2048,1024]{1,2,0:T(8,128)(2,1)}) %all-gather.6.cloned.1.call-update) | async-done | bytes 4194320 | tf_op jit(solution)/shard_map/all_gather | solution.py:73
  548.9 0.0 copy-start.1
  548.9 4.5 fusion.8
  553.4 0.0 copy-done.1
  (5 shorter events, 0.0 us)
Async XLA Ops:
  6.5 80.2 %copy-start = (bf16[1024,256]{1,0:T(8,128)(2,1)S(1)}, bf16[1024,256]{1,0:T(8,128)(2,1)}, u32[]{:S(2)}) copy-start(bf16[1024,256]{1,0:T(8,128)(2,1)} %param.10) | copy-start | bytes 1572868
  6.5 373.7 %all-gather.4.cloned.1.call-start = ((), (), s32[]{:S(2)}) async-start(), calls=%async_computation.3 | async-start | bytes 20971520 | tf_op jit(solution)/shard_map/all_gather | solution.py:34
  86.4 462.5 %all-gather.6.cloned.1.call-start = ((), (), s32[]{:S(2)}) async-start(), calls=%async_computation.4 | async-start | bytes 5242880 | tf_op jit(solution)/shard_map/all_gather | solution.py:73
  90.2 290.1 %copy-start.4 = (bf16[1024,256]{1,0:T(8,128)(2,1)S(1)}, bf16[1024,256]{1,0:T(8,128)(2,1)}, u32[]{:S(2)}) copy-start(bf16[1024,256]{1,0:T(8,128)(2,1)} %param.12) | copy-start | bytes 1572868
  419.4 3.2 copy-start.2
  454.4 5.1 copy-start.3
  548.9 4.6 copy-start.1
Sparse Core Ops, SparseCore 0:
  86.5 293.6 all-gather.3
  459.6 89.2 all-gather.5
where the time goes:
time: 561 us; the launch traced here: 560 us
  waiting for transfers between devices  358 us (64%)
  blocking collectives  88.2 us (16%)
  matrix products  48.3 us (9%)
  local copies, waits for them, and re-layouts  47 us (8%)
  between operations  13.5 us (2%)
    all_gather x1, waiting for transfers between devices, body(): block_in = lax.all_gather(arrived, 'head', axis=1, tiled=True)  285 us
    all_gather x1, waiting for transfers between devices, body(): lax.all_gather(context, 'head', axis=1, tiled=True)  72.9 us
    all_to_all x1, blocking collectives, body(): lax.all_to_all(selected, 'span', split_axis=0, concat_axis=0, tiled=True)  56.3 us
    dot_general x1, matrix products, body(): jnp.einsum('chqk,ckhd->cqhd', weights, value_rows, preferred_element_type...  22.4 us
    all_to_all x1, blocking collectives, body(): lax.all_to_all(out_weight, 'head', split_axis=1, concat_axis=0, tiled=True)  16.1 us
    all_to_all x1, blocking collectives, body(): lax.all_to_all(request, 'span', split_axis=0, concat_axis=0, tiled=True)  15.8 us
    dot_general x1, matrix products, body(): jnp.dot(flattened, both_weights, preferred_element_type=jnp.float32)  14.5 us
    unnamed x13, local copies, waits for them, and re-layouts  13.1 us
  transfers between devices with their start and end apart: 2, of which 2 were waited for; matrix products, arithmetic and copies ran while one was open for 2% of the time, Pallas kernels for 0%

commit v1 on v0

--- a/solution.py
+++ b/solution.py
@@ -70,7 +70,9 @@
     )
     context = context.reshape(-1, group_cols)
     summed = jnp.dot(
-        lax.all_gather(context, "head", axis=1, tiled=True),
+        jnp.concatenate(
+            lax.all_to_all(jnp.stack([context] * lax.axis_size("head"), 0), "head", 0, 0), 1
+        ),
         column_rows,
         preferred_element_type=jnp.float32,
     )

time: 561 us -> 571 us (1.018)
  the two profiles are of different devices: /device:TPU:33 before, /device:TPU:26 now
where the time goes in v1:
time: 571 us; the launch traced here: 570 us
  blocking collectives  250 us (44%)
  waiting for transfers between devices  199 us (35%)
  local copies, waits for them, and re-layouts  48.8 us (9%)
  matrix products  46.1 us (8%)
  between operations  13.5 us (2%)
  starting transfers between devices  7.56 us (1%)
    all_gather x1, waiting for transfers between devices, body(): block_in = lax.all_gather(arrived, 'head', axis=1, tiled=True)  199 us
    all_to_all x1, blocking collectives, body(): lax.all_to_all(jnp.stack([context] * lax.axis_size('head'), 0), 'head', 0...  179 us
    all_to_all x1, blocking collectives, body(): lax.all_to_all(selected, 'span', split_axis=0, concat_axis=0, tiled=True)  57.1 us
    dot_general x1, matrix products, body(): jnp.einsum('chqk,ckhd->cqhd', weights, value_rows, preferred_element_type...  22.4 us
    dot_general x1, matrix products, body(): jnp.dot(flattened, both_weights, preferred_element_type=jnp.float32)  14.6 us
    all_to_all x1, blocking collectives, body(): lax.all_to_all(request, 'span', split_axis=0, concat_axis=0, tiled=True)  14.2 us
    unnamed x11, local copies, waits for them, and re-layouts  14.1 us
  transfers between devices with their start and end apart: 2, of which 1 were waited for; matrix products, arithmetic and copies ran while one was open for 15% of the time, Pallas kernels for 0%

profile of v1, /device:TPU:26, one launch (start us, length us, event | category | flops | bytes accessed | tf_op | source)
XLA Modules:
  0.0 570.0 jit_solution(7651532307363425438)
XLA Ops:
  6.5 0.0 copy-start
  6.5 0.0 all-gather.2.cloned.1.call-start
  6.5 0.8 fusion.34
  7.3 0.1 copy.46
  7.4 0.1 reshape_squeeze.5
  7.5 0.2 convert_reduce_fusion
  7.7 0.1 copy.47
  7.8 0.1 broadcast_in_dim.14
  7.9 0.1 select_reduce_fusion
  8.0 0.1 copy.48
  8.1 14.2 %all_to_all.38 = s32[64,1,1]{2,1,0:T(1,128)S(1)} all-to-all(s32[64,1,1]{2,1,0:T(1,128)S(1)} %copy.48), channel_id=1, replica_groups=mesh['span'=64,'head'=4] {'span'}, dimensions={0} | all-to-all | bytes 512 | tf_op jit(solution)/shard_map/all_to_all | solution.py:28
  22.3 1.2 reduce
  23.5 4.9 gather_fusion
  28.5 57.1 %all_to_all.39 = bf16[64,32,1024]{2,1,0:T(8,128)(2,1)} all-to-all(bf16[64,32,1024]{2,1,0:T(8,128)(2,1)} %gather_fusion), channel_id=1, replica_groups=mesh['span'=64,'head'=4] {'span'}, dimensions={0} | all-to-all | bytes 8388608 | tf_op jit(solution)/shard_map/all_to_all | solution.py:33
  85.6 0.0 copy-start.3
  85.6 0.0 all-gather.2.cloned.1.call-update
  85.6 1.0 copy-done.3
  86.6 0.2 copy.55
  86.8 1.1 copy.56
  87.9 7.6 %all-to-all-start.3 = ((bf16[256,4,256]{2,0,1:T(8,128)(2,1)}), bf16[256,4,256]{2,0,1:T(8,128)(2,1)S(1)}, u32[]{:S(2)}, u32[]{:S(2)}) async-start(bf16[256,4,256]{2,0,1:T(8,128)(2,1)} %copy.56), calls=%async_computation.3 | async-start | bytes 1048576 | tf_op jit(solution)/shard_map/all_to_all | solution.py:15
  95.5 0.1 reshape_squeeze.6
  95.6 0.0 copy-done
  95.6 3.4 fusion.14
  99.0 0.2 slice.29
  99.3 1.0 concatenate.12
  100.3 3.4 reshape.102
  103.8 199.0 %all-gather.2.cloned.1.call-done = bf16[64,128,1024]{2,1,0:T(8,128)(2,1)} async-done(((bf16[64,32,1024]{2,1,0:T(8,128)(2,1)}), bf16[64,128,1024]{2,1,0:T(8,128)(2,1)}) %all-gather.2.cloned.1.call-update) | async-done | bytes 16777232 | tf_op jit(solution)/shard_map/all_gather | solution.py:34
  302.8 14.6 %convolution_convert_fusion = bf16[8192,512]{1,0:T(8,128)(2,1)} fusion(bf16[8192,1024]{1,0:T(8,128)(2,1)} %bitcast.60, bf16[1024,256]{1,0:T(8,128)(2,1)} %param.12, bf16[1024,256]{1,0:T(8,128)(2,1)} %param.11), kind=kOutput, calls=%fused_computation.3 | convolution fusion | flops 8596226048 | bytes 26214400 | tf_op jit(solution)/shard_map/dot_general | solution.py:36
  317.4 8.9 %gather_fusion.1 = bf16[64,128,512]{2,1,0:T(8,128)(2,1)} fusion(bf16[64,128,512]{2,1,0:T(8,128)(2,1)} %bitcast.55, s32[1024]{0:T(1024)S(1)} %pad_clamp_fusion), kind=kCustom, calls=%fused_computation.1 | custom fusion | bytes 16777472 | tf_op jit(solution)/shard_map/gather | solution.py:40
  326.4 5.9 %fusion.33 = (bf16[32,256,256]{2,1,0:T(8,128)(2,1)}, bf16[32,256,256]{2,1,0:T(8,128)(2,1)}) fusion(bf16[32,256,512]{2,1,0:T(8,128)(2,1)} %bitcast.53), kind=kLoop, calls=%fused_computation.40 | loop fusion | bytes 16777216 | tf_op jit(solution)/shard_map/slice | solution.py:45
  332.3 6.4 %copy.58 = bf16[32,256,256]{1,2,0:T(8,128)(2,1)} copy(bf16[32,256,256]{2,1,0:T(8,128)(2,1)} %get-tuple-element.5) | data formatting | bytes 8388608
  338.7 3.4 fusion.15
  342.1 0.0 copy-start.2
  342.1 3.1 fusion.35
  345.2 0.1 copy-done.2
  345.3 6.4 %copy.57 = bf16[32,256,256]{1,2,0:T(8,128)(2,1)} copy(bf16[32,256,256]{2,1,0:T(8,128)(2,1)} %get-tuple-element.6) | data formatting | bytes 8388608
  351.7 22.4 %convert_bitcast_fusion = bf16[32,64,4,64]{1,3,2,0:T(8,128)(2,1)} fusion(bf16[32,256,4,64]{1,3,2,0:T(8,128)(2,1)} %bitcast.57, f32[32,4,64]{2,1,0:T(4,128)S(1)} %fusion.35, f32[32,4,64,256]{3,2,1,0:T(8,128)} %copy-done.2), kind=kOutput, calls=%fused_computation.18 | convolution fusion | flops 279453952 | bytes 13664256 | tf_op jit(solution)/shard_map/chqk,ckhd->cqhd/dot_general | solution.py:63
  374.1 2.9 copy.53
  377.0 2.4 reshape.104
  379.5 1.6 pad_bitcast_fusion
  381.1 0.5 copy.54
  381.6 0.0 all-to-all-done.3
  381.7 0.3 stack.3
  381.9 0.0 copy-start.1
  381.9 179.0 %all_to_all.40 = bf16[4,2048,256]{2,1,0:T(8,128)(2,1)S(1)} all-to-all(bf16[4,2048,256]{2,1,0:T(8,128)(2,1)S(1)} %stack.3), channel_id=1, replica_groups=mesh['span'=64,'head'=4] {'head'}, dimensions={0} | all-to-all | bytes 8388608 | tf_op jit(solution)/shard_map/all_to_all | solution.py:74
  561.0 2.2 fusion.11
  563.2 0.0 copy-done.1
  (5 shorter events, 0.0 us)
Async XLA Ops:
  6.5 89.0 %copy-start = (bf16[1024,256]{1,0:T(8,128)(2,1)S(1)}, bf16[1024,256]{1,0:T(8,128)(2,1)}, u32[]{:S(2)}) copy-start(bf16[1024,256]{1,0:T(8,128)(2,1)} %param.10) | copy-start | bytes 1572868
  6.5 296.3 %all-gather.2.cloned.1.call-start = ((), (), s32[]{:S(2)}) async-start(), calls=%async_computation.4 | async-start | bytes 20971520 | tf_op jit(solution)/shard_map/all_gather | solution.py:34
  85.6 1.0 copy-start.3
  87.9 293.8 %all-to-all-start.3 = ((bf16[256,4,256]{2,0,1:T(8,128)(2,1)}), bf16[256,4,256]{2,0,1:T(8,128)(2,1)S(1)}, u32[]{:S(2)}, u32[]{:S(2)}) async-start(bf16[256,4,256]{2,0,1:T(8,128)(2,1)} %copy.56), calls=%async_computation.3 | async-start | bytes 1048576 | tf_op jit(solution)/shard_map/all_to_all | solution.py:15
  342.1 3.2 copy-start.2
  381.9 181.3 %copy-start.1 = (bf16[1024,256]{1,0:T(8,128)(2,1)S(1)}, bf16[1024,256]{1,0:T(8,128)(2,1)}, u32[]{:S(2)}) copy-start(bf16[1024,256]{1,0:T(8,128)(2,1)} %param.10) | copy-start | bytes 1572868
Sparse Core Ops, SparseCore 0:
  85.7 217.0 all-gather.1
